TPU v7x, 32 devices: a whole 2x2x4 slice. The times are simulated.
32 devices in a mesh: dp: 2 (over x), crop: 4 (over y, core), tensor: 4 (over z).
Axes of the slice: x: 2, y: 2, z: 4, core: 2. Of those that a mesh axis runs over, the one named last changes fastest.
Arguments:
- hidden_a: bfloat16 [512, 8192], P('crop', 'dp'), as said below
- hidden_b: bfloat16 [512, 8192], P('crop', 'dp'), as said below
- weight: bfloat16 [8192, 8192], P('dp', 'tensor')
Outputs:
- weight_grad: float32 [8192, 8192], P(('dp', 'crop'), 'tensor')
Inputs may be any that keep to these rules, and one draw needn't show every extreme that they name: `hidden_a`: nonnegative entries. `hidden_b`: nonnegative entries.
All inputs are finite; a program needn't handle non-finite values.
Results may differ from a plain program's by a relative error of at most 0.0015.
Values may be sent and summed in bfloat16 or wider, within the bound.
A program may use at most 128 MiB of HBM per device.

v0:
```python
import jax
import jax.numpy as jnp
from jax import lax
from jax.sharding import PartitionSpec as P

epsilon = 0.0001


def body(hidden_a, hidden_b, weight):
    group_size = lax.axis_size(("dp", "crop"))
    data_count = lax.axis_size("dp")
    block_rows = hidden_a.shape[0]
    local_rows = block_rows // data_count
    total_rows = local_rows * group_size
    left_part = jnp.dot(hidden_a, weight, preferred_element_type=jnp.float32)
    right_part = jnp.dot(hidden_b, weight, preferred_element_type=jnp.float32)
    joined = lax.psum_scatter(
        jnp.stack([left_part, right_part], axis=1), "dp", scatter_dimension=0, tiled=True
    ).astype(jnp.bfloat16)
    stacked = jnp.stack([joined[:, 0, :], joined[:, 1, :]]).astype(jnp.float32)
    col_means = lax.psum(jnp.sum(stacked, axis=1), ("dp", "crop")) / total_rows
    centered = stacked - col_means[:, None, :]
    spread = lax.psum(jnp.sum(centered * centered, axis=1), ("dp", "crop"))
    deviation = jnp.sqrt(spread / (total_rows - 1.0) + epsilon)
    rounded = centered.astype(jnp.bfloat16)
    everyone = lax.all_gather(rounded, ("dp", "crop"), axis=1, tiled=True)
    gram = jnp.einsum("vrf,vbf->vrb", rounded, everyone, preferred_element_type=jnp.float32)
    gram = lax.psum(gram, "tensor")
    gram_low = gram.astype(jnp.bfloat16)
    products = jnp.einsum("vrb,vbf->vrf", gram_low, everyone, preferred_element_type=jnp.float32)
    hinge_rate = jnp.where(deviation < 1.0, 25.0 / ((total_rows - 1.0) * deviation), 0.0)[
        :, None, :
    ]
    differ = stacked[0] - stacked[1]
    pull_term = jnp.stack([differ, -differ]) * (50.0 / total_rows)
    cov_scale = 4.0 / (total_rows - 1.0) ** 2
    row_grads = (
        pull_term - hinge_rate * centered + cov_scale * (products - centered * spread[:, None, :])
    )
    row_grads = row_grads.astype(jnp.bfloat16)
    block_grads = lax.all_gather(row_grads, "dp", axis=1, tiled=True)
    across = (((0,), (0,)), ((), ()))
    left_part = lax.dot_general(
        hidden_a, block_grads[0], across, preferred_element_type=jnp.float32
    )
    right_part = lax.dot_general(
        hidden_b, block_grads[1], across, preferred_element_type=jnp.float32
    )
    return lax.psum_scatter(left_part + right_part, "crop", scatter_dimension=0, tiled=True)


def solution(mesh):
    placed = (P("crop", "dp"), P("crop", "dp"), P("dp", "tensor"))
    return jax.shard_map(
        body, mesh=mesh, in_specs=placed, out_specs=P(("dp", "crop"), "tensor"), check_vma=False
    )
```

profile of v0, /device:TPU:0, one launch (start us, length us, event | category | flops | bytes accessed | tf_op | source)
XLA Modules:
  0.0 458.1 jit_solution(6418926525455714938)
XLA Ops:
  6.5 0.0 copy-start
  6.5 0.0 copy-start.3
  6.5 0.0 reduce-scatter.3.cloned.1.call-start
  6.5 1.2 copy-done
  7.8 0.0 copy-start.2
  7.8 8.2 %convolution_bitcast_fusion.1 = f32[128,1,2048]{2,0,1:T(8,128)S(1)} fusion(bf16[128,4096]{1,0:T(8,128)(2,1)S(1)} %copy-done, bf16[4096,2048]{1,0:T(8,128)(2,1)} %param.5), kind=kOutput, calls=%fused_computation.5 | convolution fusion | flops 2147483648 | bytes 18874368 | tf_op jit(solution)/shard_map/dot_general | solution.py:15
  16.0 0.0 copy-done.3
  16.0 2.4 copy-done.2
  18.4 2.4 convolution_bitcast_fusion
  20.8 1.5 pad_maximum_fusion
  22.3 0.0 reduce-scatter.3.cloned.1.call-update
  22.3 0.0 all-gather.3.cloned.1.call-start
  22.3 34.7 %reduce-scatter.3.cloned.1.call-done = f32[64,2,2048]{2,0,1:T(8,128)} async-done(((f32[128,2,2048]{2,0,1:T(8,128)}), f32[64,2,2048]{2,0,1:T(8,128)}) %reduce-scatter.3.cloned.1.call-update) | async-done | bytes 1048592 | tf_op jit(solution)/shard_map/reduce_scatter | solution.py:17
  57.1 1.3 convert_element_type.15
  58.4 0.1 convert_reduce_fusion
  58.5 22.9 %psum.21 = f32[2,2048]{1,0:T(2,128)S(1)} all-reduce(f32[2,2048]{1,0:T(2,128)S(1)} %convert_reduce_fusion), channel_id=1, replica_groups=mesh['dp'=2,'crop'=4,'tensor'=4] {'dp','crop'}, use_global_device_ids=true, to_apply=%region_2.0 | all-reduce | flops 4096 | bytes 32768 | tf_op jit(solution)/shard_map/psum | solution.py:21
  81.5 1.0 multiply_reduce_fusion
  82.4 0.0 all-gather.3.cloned.1.call-update
  82.4 0.0 all-gather.5.cloned.1.call-start
  82.5 22.7 %psum.22 = f32[2,2048]{1,0:T(2,128)S(1)} all-reduce(f32[2,2048]{1,0:T(2,128)S(1)} %get-tuple-element.7), channel_id=1, replica_groups=mesh['dp'=2,'crop'=4,'tensor'=4] {'dp','crop'}, use_global_device_ids=true, to_apply=%region_4.0 | all-reduce | flops 4096 | bytes 32768 | tf_op jit(solution)/shard_map/psum | solution.py:23
  105.2 0.0 copy-start.5
  105.2 0.1 fusion.6
  105.3 0.5 copy-done.5
  105.8 0.6 compare_select_fusion
  106.4 0.9 fusion.7
  107.3 12.0 %all-gather.3.cloned.1.call-done = bf16[2,512,2048]{2,1,0:T(8,128)(2,1)} async-done(((bf16[2,64,2048]{2,1,0:T(8,128)(2,1)}), bf16[2,512,2048]{2,1,0:T(8,128)(2,1)}) %all-gather.3.cloned.1.call-update) | async-done | bytes 4194320 | tf_op jit(solution)/shard_map/all_gather | solution.py:26
  119.3 3.7 fusion.8
  123.1 24.7 %all-reduce.1 = bf16[2,64,512]{2,1,0:T(8,128)(2,1)S(1)} all-reduce(f32[2,64,512]{2,1,0:T(8,128)S(1)} %fusion.8), channel_id=1, replica_groups=mesh['dp'=2,'crop'=4,'tensor'=4] {'tensor'}, use_global_device_ids=true, to_apply=%region_5.0 | all-reduce | flops 65536 | bytes 393216 | tf_op jit(solution)/shard_map/psum | solution.py:28
  147.7 4.2 fusion.2
  151.9 0.0 all-gather.5.cloned.1.call-update
  152.0 0.2 reduce-scatter.5.cloned.1.call-start
  152.2 18.8 %all-gather.5.cloned.1.call-done = bf16[2,128,2048]{2,1,0:T(8,128)(2,1)} async-done(((bf16[2,64,2048]{2,1,0:T(8,128)(2,1)}), bf16[2,128,2048]{2,1,0:T(8,128)(2,1)}) %all-gather.5.cloned.1.call-update) | async-done | bytes 1048592 | tf_op jit(solution)/shard_map/all_gather | solution.py:41
  171.0 0.0 copy-start.4
  171.0 14.3 %fusion.4 = f32[2048,4096]{1,0:T(8,128)} fusion(bf16[128,4096]{1,0:T(8,128)(2,1)S(1)} %copy-done, bf16[2,128,2048]{2,1,0:T(8,128)(2,1)} %all-gather.5.cloned.1.call-done), kind=kOutput, calls=%fused_computation.15 | convolution fusion | flops 2147483648 | bytes 35127296 | tf_op jit(solution)/shard_map/dot_general | solution.py:43
  185.3 0.0 copy-done.4
  185.3 24.8 %add_bitcast_fusion = f32[4096,2048]{0,1:T(8,128)} fusion(f32[2048,4096]{1,0:T(8,128)} %fusion.4, bf16[128,4096]{1,0:T(8,128)(2,1)S(1)} %copy-done.3, bf16[2,128,2048]{2,1,0:T(8,128)(2,1)S(1)} %copy-done.4), kind=kOutput, calls=%fused_computation | convolution fusion | flops 2155872256 | bytes 68681728 | tf_op jit(solution)/shard_map/dot_general | solution.py:46
  210.0 0.0 reduce-scatter.5.cloned.1.call-update
  210.1 0.0 copy-start.1
  210.1 232.3 %reduce-scatter.5.cloned.1.call-done = f32[1024,2048]{0,1:T(8,128)} async-done(((f32[4096,2048]{0,1:T(8,128)}), f32[1024,2048]{0,1:T(8,128)}) %reduce-scatter.5.cloned.1.call-update) | async-done | bytes 8388624 | tf_op jit(solution)/shard_map/reduce_scatter | solution.py:49
  442.4 9.1 %copy.4 = f32[1024,2048]{1,0:T(8,128)} copy(f32[1024,2048]{0,1:T(8,128)} %reduce-scatter.5.cloned.1.call-done) | data formatting | bytes 16777216 | tf_op jit(solution)/shard_map/reduce_scatter | solution.py:49
  451.5 0.0 copy-done.1
  (2 shorter events, 0.0 us)
Async XLA Ops:
  6.5 1.2 copy-start
  6.5 9.5 %copy-start.3 = (bf16[128,4096]{1,0:T(8,128)(2,1)S(1)}, bf16[128,4096]{1,0:T(8,128)(2,1)}, u32[]{:S(2)}) copy-start(bf16[128,4096]{1,0:T(8,128)(2,1)} %param.4) | copy-start | bytes 3145732
  6.5 50.5 %reduce-scatter.3.cloned.1.call-start = ((), (), s32[]{:S(2)}) async-start(), calls=%async_computation.2 | async-start | bytes 3145728 | tf_op jit(solution)/shard_map/reduce_scatter | solution.py:17
  7.8 10.6 %copy-start.2 = (bf16[4096,2048]{1,0:T(8,128)(2,1)S(1)}, bf16[4096,2048]{1,0:T(8,128)(2,1)}, u32[]{:S(2)}) copy-start(bf16[4096,2048]{1,0:T(8,128)(2,1)} %param.5) | copy-start | bytes 50331652
  22.3 97.0 %all-gather.3.cloned.1.call-start = ((), (), s32[]{:S(2)}) async-start(), calls=%async_computation.3 | async-start | bytes 4718592 | tf_op jit(solution)/shard_map/all_gather | solution.py:26
  82.4 88.5 %all-gather.5.cloned.1.call-start = ((), (), s32[]{:S(2)}) async-start(), calls=%async_computation.4 | async-start | bytes 1572864 | tf_op jit(solution)/shard_map/all_gather | solution.py:41
  105.2 0.6 copy-start.5
  152.0 290.4 %reduce-scatter.5.cloned.1.call-start = ((), (), s32[]{:S(2)}) async-start(), calls=%async_computation.5 | async-start | bytes 41943040 | tf_op jit(solution)/shard_map/reduce_scatter | solution.py:49
  171.0 14.3 %copy-start.4 = (bf16[2,128,2048]{2,1,0:T(8,128)(2,1)S(1)}, bf16[2,128,2048]{2,1,0:T(8,128)(2,1)}, u32[]{:S(2)}) copy-start(bf16[2,128,2048]{2,1,0:T(8,128)(2,1)} %all-gather.5.cloned.1.call-done) | copy-start | bytes 3145732
  210.1 241.5 %copy-start.1 = (bf16[128,4096]{1,0:T(8,128)(2,1)S(1)}, bf16[128,4096]{1,0:T(8,128)(2,1)}, u32[]{:S(2)}) copy-start(bf16[128,4096]{1,0:T(8,128)(2,1)} %param.3) | copy-start | bytes 3145732
Sparse Core Ops, SparseCore 0:
  22.4 34.6 reduce-scatter.2
  82.6 36.6 all-gather.2
  152.1 18.8 all-gather.4
  210.2 232.1 reduce-scatter.4
where the time goes:
time: 458 us
  waiting for transfers between devices  298 us (65%)
  blocking collectives  70.3 us (15%)
  matrix products  57.7 us (13%)
  local copies, waits for them, and re-layouts  13.3 us (3%)
  between operations  13.2 us (3%)
  other arithmetic  5.43 us (1%)
    reduce_scatter x1, waiting for transfers between devices, body(): lax.psum_scatter(left_part + right_part, 'crop', scatter_dimension=0, til...  232 us
    reduce_scatter x1, waiting for transfers between devices, body(): lax.psum_scatter(jnp.stack([left_part, right_part], axis=1), 'dp', scatte...  34.7 us
    dot_general x1, matrix products, body(): lax.dot_general(hidden_b, block_grads[1], across, preferred_element_type=...  24.8 us
    psum x1, blocking collectives, body(): gram = lax.psum(gram, 'tensor')  24.7 us
    psum x1, blocking collectives, body(): col_means = lax.psum(jnp.sum(stacked, axis=1), ('dp', 'crop')) / total_rows  22.9 us
    psum x1, blocking collectives, body(): spread = lax.psum(jnp.sum(centered * centered, axis=1), ('dp', 'crop'))  22.7 us
    all_gather x1, waiting for transfers between devices, body(): block_grads = lax.all_gather(row_grads, 'dp', axis=1, tiled=True)  18.8 us
    dot_general x1, matrix products, body(): lax.dot_general(hidden_a, block_grads[0], across, preferred_element_type=...  14.3 us
  transfers between devices with their start and end apart: 4, of which 4 were waited for; matrix products, arithmetic and copies ran while one was open for 0% of the time, Pallas kernels for 0%

commit v1 on v0

--- a/solution.py
+++ b/solution.py
@@ -25,7 +25,7 @@
     rounded = centered.astype(jnp.bfloat16)
     everyone = lax.all_gather(rounded, ("dp", "crop"), axis=1, tiled=True)
     gram = jnp.einsum("vrf,vbf->vrb", rounded, everyone, preferred_element_type=jnp.float32)
-    gram = lax.psum(gram, "tensor")
+    gram = jnp.sum(lax.all_gather(gram, "tensor"), axis=0)
     gram_low = gram.astype(jnp.bfloat16)
     products = jnp.einsum("vrb,vbf->vrf", gram_low, everyone, preferred_element_type=jnp.float32)
     hinge_rate = jnp.where(deviation < 1.0, 25.0 / ((total_rows - 1.0) * deviation), 0.0)[

time: 458 us -> 466 us (1.017)
  waiting for transfers between devices: 298 us -> 327 us
  blocking collectives: 70.3 us -> 47.2 us
    all_gather x1, waiting for transfers between devices: 12 us -> 36.7 us  [body(): everyone = lax.all_gather(rounded, ('dp', 'crop'), axis=1, tiled=True)]
    psum x1 -> x0, blocking collectives: 24.7 us -> none  [body(): gram = lax.psum(gram, 'tensor')]
  transfers between devices with their start and end apart: 4 -> 5, of which waited for: 4 -> 5; matrix products, arithmetic and copies ran while one was open for 0% -> 0% of each run, Pallas kernels for 0% -> 0%
where the time goes in v1:
time: 466 us; the launch traced here: 465 us
  waiting for transfers between devices  327 us (70%)
  matrix products  58.3 us (13%)
  blocking collectives  47.2 us (10%)
  between operations  13.2 us (3%)
  local copies, waits for them, and re-layouts  12.7 us (3%)
  other arithmetic  6.17 us (1%)
    reduce_scatter x1, waiting for transfers between devices, body(): lax.psum_scatter(left_part + right_part, 'crop', scatter_dimension=0, til...  232 us
    all_gather x1, waiting for transfers between devices, body(): everyone = lax.all_gather(rounded, ('dp', 'crop'), axis=1, tiled=True)  36.7 us
    reduce_scatter x1, waiting for transfers between devices, body(): lax.psum_scatter(jnp.stack([left_part, right_part], axis=1), 'dp', scatte...  34.7 us
    dot_general x1, matrix products, body(): lax.dot_general(hidden_b, block_grads[1], across, preferred_element_type=...  24.7 us
    psum x1, blocking collectives, body(): spread = lax.psum(jnp.sum(centered * centered, axis=1), ('dp', 'crop'))  24.3 us
    psum x1, blocking collectives, body(): col_means = lax.psum(jnp.sum(stacked, axis=1), ('dp', 'crop')) / total_rows  22.9 us
    all_gather x1, waiting for transfers between devices, body(): block_grads = lax.all_gather(row_grads, 'dp', axis=1, tiled=True)  20.6 us
    dot_general x1, matrix products, body(): lax.dot_general(hidden_a, block_grads[0], across, preferred_element_type=...  14.3 us
  transfers between devices with their start and end apart: 5, of which 5 were waited for; matrix products, arithmetic and copies ran while one was open for 0% of the time, Pallas kernels for 0%

profile of v1, /device:TPU:0, one launch (start us, length us, event | category | flops | bytes accessed | tf_op | source)
XLA Modules:
  0.0 465.1 jit_solution(1923657754421302038)
XLA Ops:
  6.5 0.0 copy-start
  6.5 0.0 copy-start.3
  6.5 0.0 reduce-scatter.3.cloned.1.call-start
  6.5 1.2 copy-done
  7.8 0.0 copy-start.2
  7.8 8.2 %convolution_bitcast_fusion.1 = f32[128,1,2048]{2,0,1:T(8,128)S(1)} fusion(bf16[128,4096]{1,0:T(8,128)(2,1)S(1)} %copy-done, bf16[4096,2048]{1,0:T(8,128)(2,1)} %param.5), kind=kOutput, calls=%fused_computation.5 | convolution fusion | flops 2147483648 | bytes 18874368 | tf_op jit(solution)/shard_map/dot_general | solution.py:15
  16.0 0.0 copy-done.3
  16.0 2.4 copy-done.2
  18.4 2.4 convolution_bitcast_fusion
  20.8 1.5 pad_maximum_fusion
  22.3 0.0 reduce-scatter.3.cloned.1.call-update
  22.3 0.0 all-gather.5.cloned.1.call-start
  22.3 34.7 %reduce-scatter.3.cloned.1.call-done = f32[64,2,2048]{2,0,1:T(8,128)} async-done(((f32[128,2,2048]{2,0,1:T(8,128)}), f32[64,2,2048]{2,0,1:T(8,128)}) %reduce-scatter.3.cloned.1.call-update) | async-done | bytes 1048592 | tf_op jit(solution)/shard_map/reduce_scatter | solution.py:17
  57.1 1.3 convert_element_type.15
  58.4 0.1 convert_reduce_fusion
  58.5 22.9 %psum.14 = f32[2,2048]{1,0:T(2,128)S(1)} all-reduce(f32[2,2048]{1,0:T(2,128)S(1)} %convert_reduce_fusion), channel_id=1, replica_groups=mesh['dp'=2,'crop'=4,'tensor'=4] {'dp','crop'}, use_global_device_ids=true, to_apply=%region_2.0 | all-reduce | flops 4096 | bytes 32768 | tf_op jit(solution)/shard_map/psum | solution.py:21
  81.5 1.0 multiply_reduce_fusion
  82.4 0.0 all-gather.5.cloned.1.call-update
  82.4 0.0 all-gather.9.cloned.1.call-start
  82.5 36.7 %all-gather.5.cloned.1.call-done = bf16[2,512,2048]{2,1,0:T(8,128)(2,1)} async-done(((bf16[2,64,2048]{2,1,0:T(8,128)(2,1)}), bf16[2,512,2048]{2,1,0:T(8,128)(2,1)}) %all-gather.5.cloned.1.call-update) | async-done | bytes 4194320 | tf_op jit(solution)/shard_map/all_gather | solution.py:26
  119.2 4.5 fusion.8
  123.6 0.0 all-gather.9.cloned.1.call-update
  123.7 0.0 all-gather.7.cloned.1.call-start
  123.7 24.3 %psum.15 = f32[2,2048]{1,0:T(2,128)S(1)} all-reduce(f32[2,2048]{1,0:T(2,128)S(1)} %get-tuple-element.7), channel_id=1, replica_groups=mesh['dp'=2,'crop'=4,'tensor'=4] {'dp','crop'}, use_global_device_ids=true, to_apply=%region_4.0 | all-reduce | flops 4096 | bytes 32768 | tf_op jit(solution)/shard_map/psum | solution.py:23
  148.0 0.1 fusion.6
  148.1 0.9 fusion.7
  149.0 2.8 all-gather.9.cloned.1.call-done
  151.8 1.3 reduce_sum.29
  153.1 4.2 fusion.2
  157.3 0.0 all-gather.7.cloned.1.call-update
  157.3 0.2 reduce-scatter.5.cloned.1.call-start
  157.5 20.6 %all-gather.7.cloned.1.call-done = bf16[2,128,2048]{2,1,0:T(8,128)(2,1)} async-done(((bf16[2,64,2048]{2,1,0:T(8,128)(2,1)}), bf16[2,128,2048]{2,1,0:T(8,128)(2,1)}) %all-gather.7.cloned.1.call-update) | async-done | bytes 1048592 | tf_op jit(solution)/shard_map/all_gather | solution.py:41
  178.1 0.0 copy-start.4
  178.1 14.3 %fusion.4 = f32[2048,4096]{1,0:T(8,128)} fusion(bf16[128,4096]{1,0:T(8,128)(2,1)S(1)} %copy-done, bf16[2,128,2048]{2,1,0:T(8,128)(2,1)} %all-gather.7.cloned.1.call-done), kind=kOutput, calls=%fused_computation.15 | convolution fusion | flops 2147483648 | bytes 35127296 | tf_op jit(solution)/shard_map/dot_general | solution.py:43
  192.4 0.0 copy-done.4
  192.4 24.7 %add_bitcast_fusion = f32[4096,2048]{0,1:T(8,128)} fusion(f32[2048,4096]{1,0:T(8,128)} %fusion.4, bf16[128,4096]{1,0:T(8,128)(2,1)S(1)} %copy-done.3, bf16[2,128,2048]{2,1,0:T(8,128)(2,1)S(1)} %copy-done.4), kind=kOutput, calls=%fused_computation | convolution fusion | flops 2155872256 | bytes 68681728 | tf_op jit(solution)/shard_map/dot_general | solution.py:46
  217.1 0.0 reduce-scatter.5.cloned.1.call-update
  217.2 0.0 copy-start.1
  217.2 232.3 %reduce-scatter.5.cloned.1.call-done = f32[1024,2048]{0,1:T(8,128)} async-done(((f32[4096,2048]{0,1:T(8,128)}), f32[1024,2048]{0,1:T(8,128)}) %reduce-scatter.5.cloned.1.call-update) | async-done | bytes 8388624 | tf_op jit(solution)/shard_map/reduce_scatter | solution.py:49
  449.5 9.1 %copy.5 = f32[1024,2048]{1,0:T(8,128)} copy(f32[1024,2048]{0,1:T(8,128)} %reduce-scatter.5.cloned.1.call-done) | data formatting | bytes 16777216 | tf_op jit(solution)/shard_map/reduce_scatter | solution.py:49
  458.6 0.0 copy-done.1
  (3 shorter events, 0.1 us)
Async XLA Ops:
  6.5 1.2 copy-start
  6.5 9.5 %copy-start.3 = (bf16[128,4096]{1,0:T(8,128)(2,1)S(1)}, bf16[128,4096]{1,0:T(8,128)(2,1)}, u32[]{:S(2)}) copy-start(bf16[128,4096]{1,0:T(8,128)(2,1)} %param.4) | copy-start | bytes 3145732
  6.5 50.5 %reduce-scatter.3.cloned.1.call-start = ((), (), s32[]{:S(2)}) async-start(), calls=%async_computation.2 | async-start | bytes 3145728 | tf_op jit(solution)/shard_map/reduce_scatter | solution.py:17
  7.8 10.6 %copy-start.2 = (bf16[4096,2048]{1,0:T(8,128)(2,1)S(1)}, bf16[4096,2048]{1,0:T(8,128)(2,1)}, u32[]{:S(2)}) copy-start(bf16[4096,2048]{1,0:T(8,128)(2,1)} %param.5) | copy-start | bytes 50331652
  22.3 96.9 %all-gather.5.cloned.1.call-start = ((), (), s32[]{:S(2)}) async-start(), calls=%async_computation.3 | async-start | bytes 4718592 | tf_op jit(solution)/shard_map/all_gather | solution.py:26
  82.4 69.3 %all-gather.9.cloned.1.call-start = ((), (), s32[]{:S(2)}) async-start(), calls=%async_computation.6 | async-start | bytes 1310720 | tf_op jit(solution)/shard_map/all_gather | solution.py:28
  123.7 54.5 %all-gather.7.cloned.1.call-start = ((), (), s32[]{:S(2)}) async-start(), calls=%async_computation.4 | async-start | bytes 1572864 | tf_op jit(solution)/shard_map/all_gather | solution.py:41
  157.3 292.2 %reduce-scatter.5.cloned.1.call-start = ((), (), s32[]{:S(2)}) async-start(), calls=%async_computation.5 | async-start | bytes 41943040 | tf_op jit(solution)/shard_map/reduce_scatter | solution.py:49
  178.1 14.3 %copy-start.4 = (bf16[2,128,2048]{2,1,0:T(8,128)(2,1)S(1)}, bf16[2,128,2048]{2,1,0:T(8,128)(2,1)}, u32[]{:S(2)}) copy-start(bf16[2,128,2048]{2,1,0:T(8,128)(2,1)} %all-gather.7.cloned.1.call-done) | copy-start | bytes 3145732
  217.2 241.4 %copy-start.1 = (bf16[128,4096]{1,0:T(8,128)(2,1)S(1)}, bf16[128,4096]{1,0:T(8,128)(2,1)}, u32[]{:S(2)}) copy-start(bf16[128,4096]{1,0:T(8,128)(2,1)} %param.3) | copy-start | bytes 3145732
Sparse Core Ops, SparseCore 0:
  22.4 34.6 reduce-scatter.2
  82.6 36.5 all-gather.4
  123.8 27.9 all-gather.8
  157.4 20.6 all-gather.6
  217.3 232.1 reduce-scatter.4
